TPU v7x, 32 devices: a whole 2x2x4 slice. The times are simulated.
32 devices in a mesh: front: 2 (over core), row: 4 (over y, x), col: 4 (over z).
Axes of the slice: x: 2, y: 2, z: 4, core: 2. Of those that a mesh axis runs over, the one named last changes fastest.
Arguments:
- front_rows: float32 [4096, 24576], P(('front', 'row'), 'col'), parts along dimension 0, may hold values from -0.0546875 to 0.0546875
- random_columns: bfloat16 [49152, 512], P(('front', 'col'), 'row'), parts along dimension 0, may hold values from -6 to 6
Outputs:
- basis: float32 [4096, 256], P(('front', 'row', 'col')), parts along dimension 0
- projected: float32 [1024, 512], P(('front', 'row')), parts along dimension 0
There are 2 independent parts, one for each index of `front`. A program takes and returns all parts, laid end to end along the dimension named above; each array names one. Nothing has to cross between parts.
All inputs are finite; a program needn't handle non-finite values.
Results may differ from a plain program's by a relative error of at most 0.0003.
Values may be sent and summed in bfloat16 or wider, within the bound.
A program may use at most 64 MiB of HBM per device.

v0:
```python
import jax
import jax.numpy as jnp
from jax import lax
from jax.sharding import PartitionSpec as P

RANK = 256


def partner(value, axis, stride):
    mask = 2**stride
    pairs = [(source, source ^ mask) for source in range(lax.axis_size(axis))]
    return lax.ppermute(value, axis, pairs)


def inner_rows(left, right):
    return lax.dot_general(
        left,
        right,
        (((0,), (0,)), ((), ())),
        precision=lax.Precision.HIGHEST,
        preferred_element_type=jnp.float32,
    )


def leaf_total(partial_gram):
    return partial_gram + partner(partial_gram, "row", 0)


def per_device(front_rows, random_columns):
    block_rows = front_rows.shape[0]
    col_count = lax.axis_size("col")
    col_index = lax.axis_index("col")
    row_index = lax.axis_index("row")
    own_rows = block_rows // col_count
    partial_value = jnp.dot(
        front_rows,
        lax.all_gather(random_columns, "row", axis=1, tiled=True).astype(jnp.float32),
        precision=lax.Precision.HIGHEST,
        preferred_element_type=jnp.float32,
    )
    whole = lax.psum(partial_value, "col")
    local_gram = inner_rows(whole[:, :RANK], whole)
    mine = lax.dynamic_slice_in_dim(whole, col_index * own_rows, own_rows, 0)
    gram = leaf_total(local_gram)
    lower = jnp.linalg.cholesky(gram[:, :RANK])
    basis = lax.linalg.triangular_solve(
        lower, mine[:, :RANK], left_side=False, lower=True, transpose_a=True
    )
    coupling = lax.linalg.triangular_solve(lower, gram, left_side=True, lower=True)
    half = RANK // 2
    projected = lax.dynamic_slice_in_dim(coupling, row_index % 2 * half, half, 0)
    return (basis, projected)


def solution(mesh):
    return jax.shard_map(
        per_device,
        mesh=mesh,
        in_specs=(P(("front", "row"), "col"), P(("front", "col"), "row")),
        out_specs=(P(("front", "row", "col"), None), P(("front", "row"), None)),
        check_vma=False,
    )
```

profile of v0, /device:TPU:0, one launch (start us, length us, event | category | flops | bytes accessed | tf_op | source)
XLA Modules:
  0.0 239.0 jit_solution(649683142217514492)
XLA Ops:
  7.2 0.7 all-gather.2.cloned.1.call-update
  7.9 74.5 %all-gather.2.cloned.1.call-done = bf16[6144,512]{1,0:T(8,128)(2,1)} async-done(((bf16[6144,128]{1,0:T(8,128)(2,1)}), bf16[6144,512]{1,0:T(8,128)(2,1)}) %all-gather.2.cloned.1.call-update) | async-done | bytes 6291472 | tf_op jit(solution)/shard_map/all_gather | solution.py:37
  82.4 14.8 %fusion.18 = f32[512,512]{1,0:T(8,128)} fusion(f32[512,6144]{1,0:T(8,128)} %param.2, bf16[6144,512]{1,0:T(8,128)(2,1)} %all-gather.2.cloned.1.call-done), kind=kOutput, calls=%fused_computation.41 | convolution fusion | flops 19327352832 | bytes 19922944 | tf_op jit(solution)/shard_map/dot_general | solution.py:35
  97.3 52.1 %all-reduce.3.cloned.1.call-done = f32[512,512]{1,0:T(8,128)} async-done(((f32[512,512]{1,0:T(8,128)}), f32[512,512]{1,0:T(8,128)}) %all-reduce.3.cloned.1.call-update) | async-done | bytes 1048592 | tf_op jit(solution)/shard_map/psum | solution.py:41
  149.3 3.2 %fusion = f32[256,512]{0,1:T(8,128)S(1)} fusion(f32[512,512]{1,0:T(8,128)} %all-reduce.3.cloned.1.call-done), kind=kOutput, calls=%fused_computation.4 | convolution fusion | flops 805306368 | bytes 2097152 | tf_op jit(solution)/shard_map/dot_general | solution.py:16
  152.5 1.5 collective-permute-start
  154.1 12.3 %collective-permute-done = f32[256,512]{0,1:T(8,128)S(1)} collective-permute-done((f32[256,512]{0,1:T(8,128)S(1)}, f32[256,512]{0,1:T(8,128)S(1)}, u32[]{:S(2)}, u32[]{:S(2)}) %collective-permute-start) | collective-permute-done | bytes 524320 | tf_op jit(solution)/shard_map/ppermute | solution.py:12
  166.7 11.7 %cholesky.50 = f32[128,128]{1,0:T(8,128)S(1)} custom-call(f32[128,128]{1,0:T(8,128)S(1)} %cholesky.118), custom_call_target="Cholesky" | custom-call | tf_op jit(solution)/shard_map/jit(cholesky)/cholesky | solution.py:45
  178.4 9.8 %custom-call.16 = f32[1,128,128]{1,2,0:T(8,128)S(1)} custom-call(f32[1,128,128]{2,1,0:T(8,128)S(1)} %get-tuple-element.25), custom_call_target="InvertDiagBlocksLowerTriangular" | custom-call | tf_op jit(solution)/shard_map/jit(cholesky)/cholesky | solution.py:45
  188.7 11.9 %cholesky.105 = f32[128,128]{1,0:T(8,128)S(1)} custom-call(f32[128,128]{1,0:T(8,128)S(1)} %convolution_subtract_fusion.1), custom_call_target="Cholesky" | custom-call | tf_op jit(solution)/shard_map/jit(cholesky)/cholesky | solution.py:45
  200.6 0.7 compare_reduce_fusion
  202.8 4.1 %while.1 = (s32[]{:T(128)}, f32[256,256]{1,0:T(8,128)S(1)}, s32[2,2]{1,0:T(2,128)S(1)}, f32[2,128,128]{2,1,0:T(8,128)S(1)}, s32[]{:T(128)}) while((s32[]{:T(128)}, f32[256,256]{1,0:T(8,128)S(1)}, s32[2,2]{1,0:T(2,128)S(1)}, f32[2,128,128]{2,1,0:T(8,128)S(1)}, s32[]{:T(128)}) %tuple.28), condition=%wide.while_cond, body=%wide.while_body.sunk | while | flops 2 | bytes 131181 | solution.py:46
  202.8 0.6 fusion.28
  203.4 1.4 bitcast_dynamic-update-slice_fusion.2
  204.9 0.6 fusion.28
  205.5 1.4 bitcast_dynamic-update-slice_fusion.2
  206.9 19.7 %custom-call.17 = f32[2,128,128]{1,2,0:T(8,128)S(1)} custom-call(f32[2,128,128]{2,1,0:T(8,128)S(1)} %get-tuple-element.9), custom_call_target="InvertDiagBlocksLowerTriangular" | custom-call | tf_op jit(solution)/shard_map/triangular_solve | solution.py:46
  226.6 0.4 fusion.4
  227.0 0.6 fusion.13
  227.6 0.4 fusion.3
  228.0 1.1 fusion.9
  229.2 1.1 convolution_subtract_fusion
  230.6 0.8 copy.7
  231.4 0.8 fusion.2
  (21 shorter events, 1.3 us)
Async XLA Ops:
  7.2 75.3 %all-gather.2.cloned.1.call-start = ((), (), s32[]{:S(2)}) async-start(), calls=%async_computation | async-start | bytes 7864320 | tf_op jit(solution)/shard_map/all_gather | solution.py:37
  7.9 141.4 %all-reduce.3.cloned.1.call-start = ((), (), s32[]{:S(2)}) async-start(), calls=%async_computation.1 | async-start | bytes 2097152 | tf_op jit(solution)/shard_map/psum | solution.py:41
  152.5 13.8 %collective-permute-start = (f32[256,512]{0,1:T(8,128)S(1)}, f32[256,512]{0,1:T(8,128)S(1)}, u32[]{:S(2)}, u32[]{:S(2)}) collective-permute-start(f32[256,512]{0,1:T(8,128)S(1)} %fusion), channel_id=1, source_target_pairs={{0,4},{4,0},{8,12},{12,8},{1,5},{5,1},{9,13},{13,9},{2,6},{6,2},{1... | collective-permute-start | bytes 1572872 | tf_op jit(solution)/shard_map/ppermute | solution.py:12
Sparse Core Ops, SparseCore 0:
  9.8 72.6 all-gather.1
  97.4 51.8 all-reduce.2
where the time goes:
time: 239 us
  waiting for transfers between devices  140 us (59%)
  other arithmetic  54.7 us (23%)
  matrix products  22.5 us (9%)
  between operations  15.5 us (6%)
  local copies, waits for them, and re-layouts  5.06 us (2%)
    all_gather x1, waiting for transfers between devices, per_device(): lax.all_gather(random_columns, 'row', axis=1, tiled=True)  74.5 us
    psum x1, waiting for transfers between devices, per_device(): whole = lax.psum(partial_value, 'col')  52.1 us
    another operation x6, other arithmetic, per_device(): lower = jnp.linalg.cholesky(gram[:, :RANK])  34.2 us
    another operation x4, other arithmetic, per_device(): lax.linalg.triangular_solve(lower, mine[:, :RANK], left_side=False, lower...  19.7 us
    dot_general x1, matrix products, per_device(): jnp.dot(front_rows, lax.all_gather(random_columns, 'row', axis=1, tiled=T...  14.8 us
    ppermute x1, waiting for transfers between devices, partner(): return lax.ppermute(value, axis, pairs)  12.3 us
  transfers between devices with their start and end apart: 3, of which 3 were waited for; matrix products, arithmetic and copies ran while one was open for 0% of the time, Pallas kernels for 0%

commit v1 on v0

--- a/solution.py
+++ b/solution.py
@@ -38,7 +38,7 @@
         precision=lax.Precision.HIGHEST,
         preferred_element_type=jnp.float32,
     )
-    whole = lax.psum(partial_value, "col")
+    whole = jnp.sum(lax.all_gather(partial_value, axis_name="col"), axis=0)
     local_gram = inner_rows(whole[:, :RANK], whole)
     mine = lax.dynamic_slice_in_dim(whole, col_index * own_rows, own_rows, 0)
     gram = leaf_total(local_gram)

time: 239 us -> 268 us (1.12)
  waiting for transfers between devices: 140 us -> 168 us
  matrix products: 22.5 us -> 19.4 us
  other arithmetic: 54.7 us -> 57.6 us
    all_gather x0 -> x1, waiting for transfers between devices: none -> 80.9 us  [per_device(): whole = jnp.sum(lax.all_gather(partial_value, axis_name='col'), axis=0)]
    psum x1 -> x0, waiting for transfers between devices: 52.1 us -> none  [per_device(): whole = lax.psum(partial_value, 'col')]
    reduce_sum x0 -> x1, other arithmetic: none -> 2.78 us  [per_device(): whole = jnp.sum(lax.all_gather(partial_value, axis_name='col'), axis=0)]
where the time goes in v1:
time: 268 us; the launch traced here: 267 us
  waiting for transfers between devices  168 us (63%)
  other arithmetic  57.6 us (21%)
  matrix products  19.4 us (7%)
  between operations  15.5 us (6%)
  local copies, waits for them, and re-layouts  5.06 us (2%)
    all_gather x1, waiting for transfers between devices, per_device(): whole = jnp.sum(lax.all_gather(partial_value, axis_name='col'), axis=0)  80.9 us
    all_gather x1, waiting for transfers between devices, per_device(): lax.all_gather(random_columns, 'row', axis=1, tiled=True)  74.5 us
    another operation x6, other arithmetic, per_device(): lower = jnp.linalg.cholesky(gram[:, :RANK])  34.2 us
    another operation x4, other arithmetic, per_device(): lax.linalg.triangular_solve(lower, mine[:, :RANK], left_side=False, lower...  19.7 us
    dot_general x1, matrix products, per_device(): jnp.dot(front_rows, lax.all_gather(random_columns, 'row', axis=1, tiled=T...  14.8 us
    ppermute x1, waiting for transfers between devices, partner(): return lax.ppermute(value, axis, pairs)  12.1 us
  transfers between devices with their start and end apart: 3, of which 3 were waited for; matrix products, arithmetic and copies ran while one was open for 0% of the time, Pallas kernels for 0%

profile of v1, /device:TPU:0, one launch (start us, length us, event | category | flops | bytes accessed | tf_op | source)
XLA Modules:
  0.0 267.4 jit_solution(3443054238204044259)
XLA Ops:
  7.2 0.7 all-gather.4.cloned.1.call-update
  7.9 74.5 %all-gather.4.cloned.1.call-done = bf16[6144,512]{1,0:T(8,128)(2,1)} async-done(((bf16[6144,128]{1,0:T(8,128)(2,1)}), bf16[6144,512]{1,0:T(8,128)(2,1)}) %all-gather.4.cloned.1.call-update) | async-done | bytes 6291472 | tf_op jit(solution)/shard_map/all_gather | solution.py:37
  82.4 14.8 %fusion.18 = f32[512,512]{1,0:T(8,128)} fusion(f32[512,6144]{1,0:T(8,128)} %param.2, bf16[6144,512]{1,0:T(8,128)(2,1)} %all-gather.4.cloned.1.call-done), kind=kOutput, calls=%fused_computation.41 | convolution fusion | flops 19327352832 | bytes 19922944 | tf_op jit(solution)/shard_map/dot_general | solution.py:35
  97.3 80.9 %all-gather.6.cloned.1.call-done = f32[2048,512]{1,0:T(8,128)} async-done(((f32[512,512]{1,0:T(8,128)}), f32[2048,512]{1,0:T(8,128)}) %all-gather.6.cloned.1.call-update) | async-done | bytes 4194320 | tf_op jit(solution)/shard_map/all_gather | solution.py:41
  178.2 2.8 %reduce_sum.9 = f32[512,512]{1,0:T(8,128)S(1)} reduce(f32[4,512,512]{2,1,0:T(8,128)} %bitcast.38, f32[]{:T(128)} %constant.97.clone.1), dimensions={0}, to_apply=%region_0.0 | reduce | flops 786432 | bytes 5242884 | tf_op jit(solution)/shard_map/reduce_sum | solution.py:41
  180.9 1.8 fusion
  182.8 1.5 collective-permute-start
  184.3 12.1 %collective-permute-done = f32[256,512]{0,1:T(8,128)S(1)} collective-permute-done((f32[256,512]{0,1:T(8,128)S(1)}, f32[256,512]{0,1:T(8,128)S(1)}, u32[]{:S(2)}, u32[]{:S(2)}) %collective-permute-start) | collective-permute-done | bytes 524320 | tf_op jit(solution)/shard_map/ppermute | solution.py:12
  196.7 11.7 %cholesky.50 = f32[128,128]{1,0:T(8,128)S(1)} custom-call(f32[128,128]{1,0:T(8,128)S(1)} %cholesky.118), custom_call_target="Cholesky" | custom-call | tf_op jit(solution)/shard_map/jit(cholesky)/cholesky | solution.py:45
  208.4 9.8 %custom-call.16 = f32[1,128,128]{1,2,0:T(8,128)S(1)} custom-call(f32[1,128,128]{2,1,0:T(8,128)S(1)} %get-tuple-element.25), custom_call_target="InvertDiagBlocksLowerTriangular" | custom-call | tf_op jit(solution)/shard_map/jit(cholesky)/cholesky | solution.py:45
  218.7 11.9 %cholesky.105 = f32[128,128]{1,0:T(8,128)S(1)} custom-call(f32[128,128]{1,0:T(8,128)S(1)} %convolution_subtract_fusion.1), custom_call_target="Cholesky" | custom-call | tf_op jit(solution)/shard_map/jit(cholesky)/cholesky | solution.py:45
  230.7 0.7 compare_reduce_fusion
  232.9 4.1 %while.1 = (s32[]{:T(128)}, f32[256,256]{1,0:T(8,128)S(1)}, s32[2,2]{1,0:T(2,128)S(1)}, f32[2,128,128]{2,1,0:T(8,128)S(1)}, s32[]{:T(128)}) while((s32[]{:T(128)}, f32[256,256]{1,0:T(8,128)S(1)}, s32[2,2]{1,0:T(2,128)S(1)}, f32[2,128,128]{2,1,0:T(8,128)S(1)}, s32[]{:T(128)}) %tuple.28), condition=%wide.while_cond, body=%wide.while_body.sunk | while | flops 2 | bytes 131181 | solution.py:46
  232.9 0.6 fusion.28
  233.5 1.4 bitcast_dynamic-update-slice_fusion.2
  234.9 0.6 fusion.28
  235.5 1.4 bitcast_dynamic-update-slice_fusion.2
  237.0 19.7 %custom-call.17 = f32[2,128,128]{1,2,0:T(8,128)S(1)} custom-call(f32[2,128,128]{2,1,0:T(8,128)S(1)} %get-tuple-element.9), custom_call_target="InvertDiagBlocksLowerTriangular" | custom-call | tf_op jit(solution)/shard_map/triangular_solve | solution.py:46
  256.6 0.4 fusion.4
  257.1 0.6 fusion.13
  257.7 0.4 fusion.3
  258.4 0.3 convolution_subtract_fusion
  259.0 0.8 copy.7
  259.8 0.8 fusion.2
  (22 shorter events, 1.6 us)
Async XLA Ops:
  7.2 75.3 %all-gather.4.cloned.1.call-start = ((), (), s32[]{:S(2)}) async-start(), calls=%async_computation | async-start | bytes 7864320 | tf_op jit(solution)/shard_map/all_gather | solution.py:37
  7.9 170.3 %all-gather.6.cloned.1.call-start = ((), (), s32[]{:S(2)}) async-start(), calls=%async_computation.1 | async-start | bytes 5242880 | tf_op jit(solution)/shard_map/all_gather | solution.py:41
  182.8 13.6 %collective-permute-start = (f32[256,512]{0,1:T(8,128)S(1)}, f32[256,512]{0,1:T(8,128)S(1)}, u32[]{:S(2)}, u32[]{:S(2)}) collective-permute-start(f32[256,512]{0,1:T(8,128)S(1)} %fusion), channel_id=1, source_target_pairs={{0,4},{4,0},{8,12},{12,8},{1,5},{5,1},{9,13},{13,9},{2,6},{6,2},{1... | collective-permute-start | bytes 1572872 | tf_op jit(solution)/shard_map/ppermute | solution.py:12
Sparse Core Ops, SparseCore 0:
  9.8 72.6 all-gather.3
  97.4 80.7 all-gather.5
